TPU v7x, 32 devices: a whole 2x2x4 slice. The times are simulated.
32 devices in a mesh: layer: 2 (over x), row: 4 (over z), col: 4 (over y, core).
Axes of the slice: x: 2, y: 2, z: 4, core: 2. Of those that a mesh axis runs over, the one named last changes fastest.
Arguments:
- left_matrix: float32 [2, 1024, 16384], P(None, 'row', 'col'), may hold values from -6 to 6
- right_matrix: float32 [2, 16384, 512], P(None, 'row', 'col'), may hold values from -0.03125 to 0.03125
Outputs:
- product: float32 [2, 1024, 512], P(None, 'row', 'col')
All inputs are finite; a program needn't handle non-finite values.
Results may differ from a plain program's by a relative error of at most 0.000071.
Values sent between devices are 32-bit elements; how exact they have to be, the bound alone decides.
A program may use at most 128 MiB of HBM per device.

v0:
```python
import functools

import jax
import jax.numpy as jnp
from jax import lax
from jax.experimental import pallas as pl
from jax.experimental.pallas import tpu as pltpu
from jax.sharding import PartitionSpec as P

CHUNKS = 16
MESH = pl.DeviceIdType.MESH


def kernel(rows, left, right, out, abuf, bbuf, xbuf, acc, xacc, xout, xin, pout, pin, qout, qin,
           own_sem, bsend, rsend, brecv, ysend, yrecv, xsend, xrecv, csend, crecv, psem, qsem, turn):
    x = lax.axis_index("layer")
    z = lax.axis_index("row")
    col = lax.axis_index("col")
    y = col // 2
    c = col % 2
    height = left.shape[1]
    width = right.shape[2]
    share = abuf.shape[3]
    step = share // CHUNKS
    last = rows - 1
    base = x * share
    parity = z % 2
    at_low, at_high = z == 0, z == last
    at_end = at_low | at_high
    lends = (at_low & (c == 1)) | (at_high & (c == 0))
    helps = ((z == 1) & (c == 1)) | ((z == last - 1) & (c == 0))
    inward = jnp.where(at_low, 1, last - 1)
    outward = jnp.where(z == 1, 0, last)
    lent_slot = jnp.where(at_low, 0, (last - 1) // 2)
    lends_own = lends & (y == lent_slot)
    lends_relayed = lends & (y != lent_slot)

    def other(**where):
        return dict(device_id=where, device_id_type=MESH)

    partner = dict(col=y * 2 + 1 - c)
    across = dict(col=(1 - y) * 2 + c)
    copy_x = dict(layer=1 - x)

    barrier = pltpu.get_barrier_semaphore()
    for where in (partner, across, copy_x):
        pl.semaphore_signal(barrier, inc=1, **other(**where))

    @pl.when(z > 0)
    def _():
        for core in range(2):
            pl.semaphore_signal(barrier, inc=1, **other(row=z - 1, col=y * 2 + core))

    @pl.when(z < last)
    def _():
        for core in range(2):
            pl.semaphore_signal(barrier, inc=1, **other(row=z + 1, col=y * 2 + core))

    own_copy = pltpu.make_async_copy(left.at[:, :, pl.ds(base, share)], abuf.at[y], own_sem)
    own_copy.start()
    acc[...] = jnp.zeros_like(acc)
    xacc[...] = jnp.zeros_like(xacc)
    pl.semaphore_wait(barrier, 3 + 2 * ((z > 0).astype(jnp.int32) + (z < last).astype(jnp.int32)))

    def span(i):
        return pl.ds(pl.multiple_of(i * step, step), step)

    def source_span(i):
        return pl.ds(pl.multiple_of(base + i * step, step), step)

    def half(h):
        return pl.ds(pl.multiple_of(h * width, width), width)

    def b_copy(i, way, row):
        return pltpu.make_async_remote_copy(
            src_ref=right.at[:, source_span(i), :],
            dst_ref=bbuf.at[z // 2, c, :, span(i), :],
            send_sem=bsend.at[way, i], recv_sem=brecv.at[z // 2, c, i],
            **other(row=row, col=y * 2 + parity))

    def b_local(i):
        return pltpu.make_async_copy(
            right.at[:, source_span(i), :], bbuf.at[z // 2, c, :, span(i), :],
            brecv.at[z // 2, c, i])

    def y_copy(i):
        return pltpu.make_async_remote_copy(
            src_ref=left.at[:, :, source_span(i)], dst_ref=abuf.at[y, :, :, span(i)],
            send_sem=ysend.at[i], recv_sem=yrecv.at[i], **other(**across))

    def y_arrival(i):
        return pltpu.make_async_remote_copy(
            src_ref=left.at[:, :, source_span(i)], dst_ref=abuf.at[1 - y, :, :, span(i)],
            send_sem=ysend.at[i], recv_sem=yrecv.at[i], **other(**across))

    def x_own(i):
        return pltpu.make_async_remote_copy(
            src_ref=left.at[:, :, source_span(i)], dst_ref=xbuf.at[:, :, span(i)],
            send_sem=xsend.at[i], recv_sem=xrecv.at[i], **other(row=inward))

    def x_relay(i):
        return pltpu.make_async_remote_copy(
            src_ref=abuf.at[1 - y, :, :, span(i)], dst_ref=xbuf.at[:, :, span(i)],
            send_sem=xsend.at[i], recv_sem=xrecv.at[i], **other(row=inward))

    yields = at_end & jnp.logical_not(lends) & (y == lent_slot)
    sends_up = (z < last) & (z != last - 1)
    sends_down = (z > 0) & (z != 1)

    def launch(i, carry):
        @pl.when(sends_up)
        def _():
            b_copy(i, 0, z + 1).start()

        @pl.when(sends_down)
        def _():
            b_copy(i, 1, z - 1).start()

        @pl.when(jnp.logical_not(yields))
        def _():
            y_copy(i).start()

        @pl.when(c == parity)
        def _():
            b_local(i).start()

        @pl.when(c != parity)
        def _():
            b_copy(i, 2, z).start()

        return carry

    lax.fori_loop(0, CHUNKS, launch, 0)

    @pl.when(lends_own)
    def _():
        def lend(i, carry):
            x_own(i).start()
            return carry
        lax.fori_loop(0, CHUNKS, lend, 0)

    @pl.when(lends_own)
    def _():
        def crossed(i, carry):
            y_copy(i).wait_send()
            return carry
        lax.fori_loop(0, CHUNKS - 1, crossed, 0)
        pl.semaphore_signal(turn, inc=1, **other(**partner))

    @pl.when(yields)
    def _():
        pl.semaphore_wait(turn, 1)

        def cross(i, carry):
            y_copy(i).start()
            return carry
        lax.fori_loop(0, CHUNKS, cross, 0)

    own_copy.wait()

    def b_arrival(s, h, i):
        ref = bbuf.at[s, h, :, span(i), :]
        return pltpu.make_async_copy(ref, ref, brecv.at[s, h, i])

    def relay(s, h, i, row):
        ref = bbuf.at[s, h, :, span(i), :]
        return pltpu.make_async_remote_copy(
            src_ref=ref, dst_ref=ref, send_sem=rsend.at[s, h, i], recv_sem=brecv.at[s, h, i],
            **other(row=row))

    def present(s):
        quarter = 2 * s + c
        return jnp.logical_not((at_low & (quarter == 1)) | (at_high & (quarter == last - 1)))

    def goes_up(s):
        quarter = 2 * s + c
        return (quarter < z) & (z < last)

    def goes_down(s):
        quarter = 2 * s + c
        return (quarter > z) & (z > 0)

    def split(value):
        high = value.astype(jnp.bfloat16)
        return high, (value - high.astype(jnp.float32)).astype(jnp.bfloat16)

    def dot(a, b):
        a_high, a_low = split(a)
        b_high, b_low = split(b)
        return jnp.dot(
            jnp.concatenate([a_high, a_high, a_low], axis=1),
            jnp.concatenate([b_high, b_low, b_high], axis=0),
            preferred_element_type=jnp.float32)

    def multiply(totals, a_ref, s, i):
        @pl.when(i % 2 == 1)
        def _():
            at = pl.ds(pl.multiple_of((i - 1) * step, 2 * step), 2 * step)
            a_re, a_im = a_ref[0, :, at], a_ref[1, :, at]
            b_re, b_im = (
                jnp.concatenate([bbuf[s, h, k, at, :] for h in range(2)], axis=1)
                for k in range(2))
            totals[0] += dot(a_re, b_re)
            totals[1] += dot(a_im, b_im)
            totals[2] += dot(a_re + a_im, b_re + b_im)

    def right_step(i):
        for s in range(2):
            @pl.when(present(s))
            def _():
                for h in range(2):
                    b_arrival(s, h, i).wait()

                    @pl.when(goes_up(s))
                    def _():
                        relay(s, h, i, z + 1).start()

                    @pl.when(goes_down(s))
                    def _():
                        relay(s, h, i, z - 1).start()

        @pl.when(present(y))
        def _():
            multiply(acc, abuf.at[y], y, i)

    def left_step(i):
        y_arrival(i).wait_recv()

        @pl.when(lends_relayed)
        def _():
            x_relay(i).start()

        @pl.when(present(1 - y))
        def _():
            multiply(acc, abuf.at[1 - y], 1 - y, i)

        @pl.when(helps)
        def _():
            x_own(i).wait_recv()
            multiply(xacc, xbuf, z // 2, i)

    early = jnp.logical_not(at_end) & (c != parity)

    def work(t, carry):
        first = t < CHUNKS
        apart = jnp.where(first, t, t - CHUNKS)
        i = jnp.where(early | lends_relayed, apart, t // 2)
        is_left = ((early & jnp.logical_not(first)) | (lends_relayed & first)
                   | (jnp.logical_not(early | lends_relayed) & (t % 2 == 1)))

        @pl.when(is_left)
        def _():
            left_step(i)

        @pl.when(jnp.logical_not(is_left))
        def _():
            right_step(i)

        return carry

    lax.fori_loop(0, 2 * CHUNKS, work, 0)

    def combined(totals, h):
        first, second, third = (totals[k, :, half(h)] for k in range(3))
        return first - second, third - first - second

    def lend_back(h):
        return pltpu.make_async_remote_copy(
            src_ref=xout.at[h], dst_ref=xin, send_sem=csend.at[h], recv_sem=crecv,
            **other(row=outward, col=y * 2 + h))

    @pl.when(helps)
    def _():
        for h in range(2):
            xout[h, 0], xout[h, 1] = combined(xacc, h)
        for h in range(2):
            lend_back(h).start()

    pout[0], pout[1] = combined(acc, 1 - c)
    to_partner = pltpu.make_async_remote_copy(
        src_ref=pout, dst_ref=pin, send_sem=psem.at[0], recv_sem=psem.at[1], **other(**partner))
    to_partner.start()
    mine_re, mine_im = combined(acc, c)
    qout[0] = mine_re
    qout[1] = mine_im
    to_partner.wait_recv()
    qout[...] += pin[...]

    @pl.when(at_end)
    def _():
        pltpu.make_async_copy(xin, xin, crecv).wait()
        qout[...] += xin[...]

    to_copy = pltpu.make_async_remote_copy(
        src_ref=qout, dst_ref=qin, send_sem=qsem.at[0], recv_sem=qsem.at[1], **other(**copy_x))
    to_copy.start()

    def settle(i, carry):
        @pl.when(sends_up)
        def _():
            b_copy(i, 0, z).wait_send()

        @pl.when(sends_down)
        def _():
            b_copy(i, 1, z).wait_send()

        @pl.when(c != parity)
        def _():
            b_copy(i, 2, z).wait_send()

        @pl.when(jnp.logical_not(lends_own & (i < CHUNKS - 1)))
        def _():
            y_copy(i).wait_send()

        @pl.when(lends)
        def _():
            x_own(i).wait_send()

        for s in range(2):
            @pl.when(present(s) & (goes_up(s) | goes_down(s)))
            def _():
                for h in range(2):
                    relay(s, h, i, z).wait_send()

        return carry

    lax.fori_loop(0, CHUNKS, settle, 0)

    @pl.when(helps)
    def _():
        for h in range(2):
            lend_back(h).wait_send()

    to_partner.wait_send()
    to_copy.wait()
    out[...] = qout[...] + qin[...]


def lent_product(left_matrix, right_matrix, layers, rows):
    height = left_matrix.shape[1]
    width = right_matrix.shape[2]
    share = left_matrix.shape[2] // layers
    f32 = jnp.float32
    dma = pltpu.SemaphoreType.DMA
    block = (2, height, width)
    return pl.pallas_call(
        functools.partial(kernel, rows),
        out_shape=jax.ShapeDtypeStruct(block, f32),
        in_specs=[pl.BlockSpec(memory_space=pl.ANY)] * 2,
        out_specs=pl.BlockSpec(memory_space=pltpu.VMEM),
        scratch_shapes=[
            pltpu.VMEM((2, 2, height, share), f32),
            pltpu.VMEM((2, 2, 2, share, width), f32),
            pltpu.VMEM((2, height, share), f32),
            pltpu.VMEM((3, height, 2 * width), f32),
            pltpu.VMEM((3, height, 2 * width), f32),
            pltpu.VMEM((2,) + block, f32),
            pltpu.VMEM(block, f32),
            pltpu.VMEM(block, f32),
            pltpu.VMEM(block, f32),
            pltpu.VMEM(block, f32),
            pltpu.VMEM(block, f32),
            dma,
            dma((3, CHUNKS)),
            dma((2, 2, CHUNKS)),
            dma((2, 2, CHUNKS)),
            dma((CHUNKS,)),
            dma((CHUNKS,)),
            dma((CHUNKS,)),
            dma((CHUNKS,)),
            dma((2,)),
            dma,
            dma((2,)),
            dma((2,)),
            pltpu.SemaphoreType.REGULAR,
        ],
        compiler_params=pltpu.CompilerParams(
            collective_id=0, has_side_effects=True, vmem_limit_bytes=60 * 2**20),
    )(left_matrix, right_matrix)


def gathered_product(left_matrix, right_matrix, layers):
    layer_index = lax.axis_index("layer")
    local_cols = right_matrix.shape[2]
    left_width = left_matrix.shape[2]
    right_height = right_matrix.shape[1]
    share_width = left_width // layers
    group_count = right_height // left_width
    left_own = lax.dynamic_slice_in_dim(left_matrix, layer_index * share_width, share_width, 2)
    right_view = right_matrix.reshape(2, group_count, layers, share_width, local_cols)
    right_own = lax.dynamic_slice_in_dim(right_view, layer_index, 1, 2)
    right_own = right_own.reshape(2, group_count * share_width, local_cols)
    right_whole = lax.all_gather(right_own, "row", axis=1, tiled=True)
    left_whole = lax.all_gather(left_own, "col", axis=2, tiled=True)
    dot = functools.partial(
        jnp.dot, precision=lax.Precision.HIGHEST, preferred_element_type=jnp.float32)
    first_term = dot(left_whole[0], right_whole[0])
    second_term = dot(left_whole[1], right_whole[1])
    third_term = dot(left_whole[0] + left_whole[1], right_whole[0] + right_whole[1])
    partial_product = jnp.stack([first_term - second_term, third_term - first_term - second_term])
    return lax.psum(partial_product, "layer")


def local(left_matrix, right_matrix):
    layers = lax.axis_size("layer")
    rows = lax.axis_size("row")
    cols = lax.axis_size("col")
    if layers == 2 and rows == cols == 4:
        return lent_product(left_matrix, right_matrix, layers, rows)
    return gathered_product(left_matrix, right_matrix, layers)


def solution(mesh):
    in_specs = (P(None, "row", "col"), P(None, "row", "col"))
    out_specs = P(None, "row", "col")
    return jax.shard_map(local, mesh=mesh, in_specs=in_specs, out_specs=out_specs, check_vma=False)
```

profile of v0, /device:TPU:0, one launch (start us, length us, event | category | flops | bytes accessed | tf_op | source)
XLA Modules:
  0.0 116.1 jit_solution(9828717473592760929)
XLA Ops:
  0.0 114.4 %shard_map.28 = f32[2,256,128]{2,1,0:T(8,128)} custom-call(f32[2,256,4096]{2,1,0:T(8,128)} %left.1, f32[2,4096,128]{2,1,0:T(8,128)} %right.1), custom_call_target="tpu_custom_call" | custom-call | tf_op jit(solution)/shard_map/pallas_call | solution.py:346
  114.4 1.7 %copy.4 = f32[2,256,128]{2,1,0:T(8,128)} copy(f32[2,256,128]{2,1,0:T(8,128)} %shard_map.28) | data formatting | bytes 524288
where the time goes:
time: 118 us; the launch traced here: 116 us
  Pallas kernels  114 us (97%)
  local copies, waits for them, and re-layouts  1.67 us (1%)
    pallas_call x1, Pallas kernels, lent_product(): pl.pallas_call(functools.partial(kernel, rows), out_shape=jax.ShapeDtypeS...  114 us

commit v1 on v0

v1 whole, which is shorter than its diff:
```python
import functools

import jax
import jax.numpy as jnp
from jax import lax
from jax.experimental import pallas as pl
from jax.experimental.pallas import tpu as pltpu
from jax.sharding import PartitionSpec as P

CHUNKS = 16
FINE = 2
GROUPS = 4
MESH = pl.DeviceIdType.MESH


def kernel(rows, left, right, out, abuf, bbuf, xbuf, ebuf, acc, xacc, xout, xin, pout, pin, qout, qin,
           own_sem, bsend, rsend, brecv, bown, ysend, yrecv, xsend, xrecv, esem, csend, crecv,
           psend, precv, qsend, qrecv, turn):
    x = lax.axis_index("layer")
    z = lax.axis_index("row")
    col = lax.axis_index("col")
    y = col // 2
    c = col % 2
    height = left.shape[1]
    width = right.shape[2]
    share = abuf.shape[3]
    step = share // CHUNKS
    fine = step // FINE
    tall = height // GROUPS
    wide = share // GROUPS
    last = rows - 1
    tail = CHUNKS - 1
    base = x * share
    parity = z % 2
    at_low, at_high = z == 0, z == last
    at_end = at_low | at_high
    lends = (at_low & (c == 1)) | (at_high & (c == 0))
    helps = ((z == 1) & (c == 1)) | ((z == last - 1) & (c == 0))
    inward = jnp.where(at_low, 1, last - 1)
    outward = jnp.where(z == 1, 0, last)
    far = jnp.where(z < rows // 2, last, 0)
    lent_slot = jnp.where(at_low, 0, (last - 1) // 2)
    lends_own = lends & (y == lent_slot)
    lends_relayed = lends & (y != lent_slot)

    def other(**where):
        return dict(device_id=where, device_id_type=MESH)

    partner = dict(col=y * 2 + 1 - c)
    across = dict(col=(1 - y) * 2 + c)
    copy_x = dict(layer=1 - x)

    barrier = pltpu.get_barrier_semaphore()
    for where in (partner, across, copy_x):
        pl.semaphore_signal(barrier, inc=1, **other(**where))

    @pl.when(z > 0)
    def _():
        for core in range(2):
            pl.semaphore_signal(barrier, inc=1, **other(row=z - 1, col=y * 2 + core))

    @pl.when(z < last)
    def _():
        for core in range(2):
            pl.semaphore_signal(barrier, inc=1, **other(row=z + 1, col=y * 2 + core))

    own_copy = pltpu.make_async_copy(left.at[:, :, pl.ds(base, share)], abuf.at[y], own_sem)
    own_copy.start()
    acc[...] = jnp.zeros_like(acc)
    xacc[...] = jnp.zeros_like(xacc)
    pl.semaphore_wait(barrier, 3 + 2 * ((z > 0).astype(jnp.int32) + (z < last).astype(jnp.int32)))

    def span(i):
        return pl.ds(pl.multiple_of(i * step, step), step)

    def source_span(i):
        return pl.ds(pl.multiple_of(base + i * step, step), step)

    def fine_span(u):
        return pl.ds(pl.multiple_of(u * fine, fine), fine)

    def fine_source(u):
        return pl.ds(pl.multiple_of(base + u * fine, fine), fine)

    def half(h):
        return pl.ds(pl.multiple_of(h * width, width), width)

    def group(g):
        return pl.ds(pl.multiple_of(g * tall, tall), tall)

    def piece_rows(i):
        return group(i // GROUPS)

    def piece_cols(i):
        return pl.ds(pl.multiple_of((i % GROUPS) * wide, wide), wide)

    def piece_source(i):
        return pl.ds(pl.multiple_of(base + (i % GROUPS) * wide, step), wide)

    whole_source = pl.ds(pl.multiple_of(base, step), share)

    def b_copy(u, way, row):
        return pltpu.make_async_remote_copy(
            src_ref=right.at[:, fine_source(u), :],
            dst_ref=bbuf.at[z // 2, c, :, fine_span(u), :],
            send_sem=bsend.at[way], recv_sem=brecv.at[z // 2, u],
            **other(row=row, col=y * 2 + parity))

    def b_sent(way):
        return pltpu.make_async_remote_copy(
            src_ref=right.at[:, whole_source, :], dst_ref=bbuf.at[z // 2, c],
            send_sem=bsend.at[way], recv_sem=bown.at[1], **other(**partner))

    b_local = pltpu.make_async_copy(right.at[:, whole_source, :], bbuf.at[z // 2, c], bown.at[0])
    b_partner = b_sent(2)

    def y_part(i):
        return (i == tail).astype(jnp.int32) if not isinstance(i, int) else int(i == tail)

    def y_copy(i):
        return pltpu.make_async_remote_copy(
            src_ref=left.at[:, :, source_span(i)], dst_ref=abuf.at[y, :, :, span(i)],
            send_sem=ysend.at[y_part(i)], recv_sem=yrecv.at[i], **other(**across))

    def y_piece(i):
        return pltpu.make_async_remote_copy(
            src_ref=left.at[:, piece_rows(i), piece_source(i)],
            dst_ref=abuf.at[y, :, piece_rows(i), piece_cols(i)],
            send_sem=ysend.at[y_part(i)], recv_sem=yrecv.at[i], **other(**across))

    def y_sent(part):
        size = (tail if part == 0 else 1) * step
        ref = abuf.at[y, :, :, pl.ds(0, size)]
        return pltpu.make_async_remote_copy(
            src_ref=ref, dst_ref=ref, send_sem=ysend.at[part], recv_sem=yrecv.at[0], **other(**across))

    def y_arrival(i):
        ref = abuf.at[1 - y, :, :, span(i)]
        return pltpu.make_async_copy(ref, ref, yrecv.at[i])

    def y_piece_arrival(i):
        ref = abuf.at[1 - y, :, piece_rows(i), piece_cols(i)]
        return pltpu.make_async_copy(ref, ref, yrecv.at[i])

    def x_own(i):
        return pltpu.make_async_remote_copy(
            src_ref=left.at[:, piece_rows(i), piece_source(i)],
            dst_ref=xbuf.at[:, piece_rows(i), piece_cols(i)],
            send_sem=xsend, recv_sem=xrecv.at[i], **other(row=inward))

    def x_relay(i):
        return pltpu.make_async_remote_copy(
            src_ref=abuf.at[1 - y, :, piece_rows(i), piece_cols(i)],
            dst_ref=xbuf.at[:, piece_rows(i), piece_cols(i)],
            send_sem=xsend, recv_sem=xrecv.at[i], **other(row=inward))

    def x_arrival(i):
        ref = xbuf.at[:, piece_rows(i), piece_cols(i)]
        return pltpu.make_async_copy(ref, ref, xrecv.at[i])

    x_sent = pltpu.make_async_remote_copy(
        src_ref=xbuf, dst_ref=xbuf, send_sem=xsend, recv_sem=xrecv.at[0], **other(row=inward))
    e_own = pltpu.make_async_remote_copy(
        src_ref=left.at[:, :, source_span(tail)], dst_ref=ebuf,
        send_sem=esem.at[0], recv_sem=esem.at[1], **other(row=inward))
    e_relay = pltpu.make_async_remote_copy(
        src_ref=abuf.at[1 - y, :, :, span(tail)], dst_ref=ebuf,
        send_sem=esem.at[0], recv_sem=esem.at[1], **other(row=inward))

    yields = at_end & jnp.logical_not(lends) & (y == lent_slot)
    sends_up = (z < last) & (z != last - 1)
    sends_down = (z > 0) & (z != 1)

    @pl.when(lends_relayed)
    def _():
        y_copy(tail).start()

    def launch(i, carry):
        for k in range(FINE):
            @pl.when(sends_up)
            def _():
                b_copy(i * FINE + k, 0, z + 1).start()

            @pl.when(sends_down)
            def _():
                b_copy(i * FINE + k, 1, z - 1).start()

        @pl.when(jnp.logical_not(yields | lends_own) & jnp.logical_not(lends_relayed & (i == tail)))
        def _():
            y_copy(i).start()

        @pl.when(lends_own)
        def _():
            y_piece(i).start()

        return carry

    lax.fori_loop(0, CHUNKS, launch, 0)

    @pl.when(c == parity)
    def _():
        b_local.start()

    @pl.when(c != parity)
    def _():
        b_partner.start()

    @pl.when(lends_relayed)
    def _():
        e_own.start()

    @pl.when(lends_own)
    def _():
        y_arrival(tail).wait()
        e_relay.start()

        def lend(i, carry):
            x_own(i).start()
            return carry
        lax.fori_loop(0, CHUNKS, lend, 0)
        y_sent(0).wait_send()
        pl.semaphore_signal(turn, inc=1, **other(**partner))

    @pl.when(yields)
    def _():
        pl.semaphore_wait(turn, 1)

        def cross(i, carry):
            y_copy(i).start()
            return carry
        lax.fori_loop(0, CHUNKS, cross, 0)

    own_copy.wait()

    @pl.when(c == parity)
    def _():
        b_local.wait()
        b_sent(2).wait_recv()

    def b_arrival(s, u):
        ref = bbuf.at[s, :, :, fine_span(u), :]
        return pltpu.make_async_copy(ref, ref, brecv.at[s, u])

    def relay(s, u, part, row):
        ref = bbuf.at[s, :, :, fine_span(u), :]
        return pltpu.make_async_remote_copy(
            src_ref=ref, dst_ref=ref, send_sem=rsend.at[s, part], recv_sem=brecv.at[s, u],
            **other(row=row))

    def relayed(s, part):
        start, size = ((0, tail) if part == 0 else (tail, 1))
        ref = bbuf.at[s, :, :, pl.ds(start * step, size * step), :]
        return pltpu.make_async_remote_copy(
            src_ref=ref, dst_ref=ref, send_sem=rsend.at[s, part], recv_sem=brecv.at[s, 0],
            **other(row=inward))

    def present(s):
        quarter = 2 * s + c
        return jnp.logical_not((at_low & (quarter == 1)) | (at_high & (quarter == last - 1)))

    def is_own(s):
        return 2 * s + c == z

    def is_far(s):
        return 2 * s + c == far

    def goes_up(s):
        quarter = 2 * s + c
        return (quarter < z) & (z < last)

    def goes_down(s):
        quarter = 2 * s + c
        return (quarter > z) & (z > 0)

    def goes(s, i):
        cut = is_far(s) & ((z == 1) | (z == last - 1)) & (i == tail)
        return (goes_up(s) | goes_down(s)) & jnp.logical_not(cut)

    def split(value):
        high = value.astype(jnp.bfloat16)
        return high, (value - high.astype(jnp.float32)).astype(jnp.bfloat16)

    def dot(a, b):
        a_high, a_low = split(a)
        b_high, b_low = split(b)
        return jnp.dot(
            jnp.concatenate([a_high, a_high, a_low], axis=1),
            jnp.concatenate([b_high, b_low, b_high], axis=0),
            preferred_element_type=jnp.float32)

    def both(s, at):
        return (jnp.concatenate([bbuf[s, h, k, at, :] for h in range(2)], axis=1) for k in range(2))

    def multiply(a_ref, s, i):
        def add(at):
            a_re, a_im = a_ref[0, :, at], a_ref[1, :, at]
            b_re, b_im = both(s, at)
            acc[0] += dot(a_re, b_re)
            acc[1] += dot(a_im, b_im)
            acc[2] += dot(a_re + a_im, b_re + b_im)

        alone = at_end & is_far(s) & (i == tail)

        @pl.when((i % 2 == 1) & jnp.logical_not(alone))
        def _():
            add(pl.ds(pl.multiple_of((i - 1) * step, 2 * step), 2 * step))

        @pl.when(alone)
        def _():
            add(span(i - 1))

    def lent_multiply(i):
        at, band = piece_cols(i), piece_rows(i)
        a_re, a_im = xbuf[0, band, at], xbuf[1, band, at]
        b_re, b_im = both(z // 2, at)
        xacc[0, band] += dot(a_re, b_re)
        xacc[1, band] += dot(a_im, b_im)
        xacc[2, band] += dot(a_re + a_im, b_re + b_im)

    def right_step(i):
        for s in range(2):
            @pl.when(present(s) & jnp.logical_not(is_own(s)) & jnp.logical_not(at_end & is_far(s) & (i == tail)))
            def _():
                for k in range(FINE):
                    b_arrival(s, i * FINE + k).wait()

                    @pl.when(goes(s, i))
                    def _():
                        relay(s, i * FINE + k, (i == tail).astype(jnp.int32),
                              jnp.where(goes_up(s), z + 1, z - 1)).start()

        @pl.when(present(y))
        def _():
            multiply(abuf.at[y], y, i)

    def left_step(i):
        @pl.when(jnp.logical_not(lends_relayed | (lends_own & (i == tail))))
        def _():
            y_arrival(i).wait()

        @pl.when(lends_relayed)
        def _():
            y_piece_arrival(i).wait()
            x_relay(i).start()

        @pl.when(present(1 - y))
        def _():
            multiply(abuf.at[1 - y], 1 - y, i)

        @pl.when(helps)
        def _():
            x_arrival(i).wait()
            lent_multiply(i)

    early = jnp.logical_not(at_end) & (c != parity)

    def work(t, carry):
        first = t < CHUNKS
        apart = jnp.where(first, t, t - CHUNKS)
        i = jnp.where(early | lends_relayed, apart, t // 2)
        is_left = ((early & jnp.logical_not(first)) | (lends_relayed & first)
                   | (jnp.logical_not(early | lends_relayed) & (t % 2 == 1)))

        @pl.when(is_left)
        def _():
            left_step(i)

        @pl.when(jnp.logical_not(is_left))
        def _():
            right_step(i)

        return carry

    lax.fori_loop(0, 2 * CHUNKS, work, 0)

    def combined(totals, h, g):
        first, second, third = (totals[k, group(g), half(h)] for k in range(3))
        return first - second, third - first - second

    def lend_back(h, g):
        return pltpu.make_async_remote_copy(
            src_ref=xout.at[h, :, group(g)], dst_ref=xin.at[:, group(g)],
            send_sem=csend.at[h], recv_sem=crecv.at[g], **other(row=outward, col=y * 2 + h))

    def lent_back(h):
        return pltpu.make_async_remote_copy(
            src_ref=xout.at[h], dst_ref=xin, send_sem=csend.at[h], recv_sem=crecv.at[0],
            **other(row=outward, col=y * 2 + h))

    def lent_arrival(g):
        ref = xin.at[:, group(g)]
        return pltpu.make_async_copy(ref, ref, crecv.at[g])

    @pl.when(helps)
    def _():
        e_own.wait_recv()
        at = span(tail)

        def give(g, carry):
            band = group(g)
            a_re, a_im = ebuf[0, band, :], ebuf[1, band, :]
            b_re, b_im = both(1 - z // 2, at)
            xacc[0, band] += dot(a_re, b_re)
            xacc[1, band] += dot(a_im, b_im)
            xacc[2, band] += dot(a_re + a_im, b_re + b_im)
            for h in range(2):
                xout[h, 0, band], xout[h, 1, band] = combined(xacc, h, g)
            for h in range(2):
                lend_back(h, g).start()
            return carry

        lax.fori_loop(0, GROUPS, give, 0)

    def to_partner(g):
        return pltpu.make_async_remote_copy(
            src_ref=pout.at[:, group(g)], dst_ref=pin.at[:, group(g)],
            send_sem=psend, recv_sem=precv.at[g], **other(**partner))

    def to_copy(g):
        return pltpu.make_async_remote_copy(
            src_ref=qout.at[:, group(g)], dst_ref=qin.at[:, group(g)],
            send_sem=qsend, recv_sem=qrecv.at[g], **other(**copy_x))

    def hand(g, carry):
        pout[0, group(g)], pout[1, group(g)] = combined(acc, 1 - c, g)
        to_partner(g).start()
        return carry

    lax.fori_loop(0, GROUPS, hand, 0)

    def gather(g, carry):
        band = group(g)
        mine_re, mine_im = combined(acc, c, g)
        to_partner(g).wait_recv()
        qout[0, band] = mine_re + pin[0, band]
        qout[1, band] = mine_im + pin[1, band]

        @pl.when(at_end)
        def _():
            lent_arrival(g).wait()
            qout[:, band] += xin[:, band]

        to_copy(g).start()
        return carry

    lax.fori_loop(0, GROUPS, gather, 0)

    @pl.when(sends_up)
    def _():
        b_sent(0).wait_send()

    @pl.when(sends_down)
    def _():
        b_sent(1).wait_send()

    @pl.when(c != parity)
    def _():
        b_partner.wait_send()

    @pl.when(jnp.logical_not(lends_own))
    def _():
        y_sent(0).wait_send()

    y_sent(1).wait_send()

    @pl.when(lends)
    def _():
        x_sent.wait_send()
        e_own.wait_send()

    for s in range(2):
        for part in range(2):
            @pl.when(present(s) & goes(s, tail * part))
            def _():
                relayed(s, part).wait_send()

    @pl.when(helps)
    def _():
        for h in range(2):
            lent_back(h).wait_send()

    whole_part = pltpu.make_async_remote_copy(
        src_ref=pout, dst_ref=pin, send_sem=psend, recv_sem=precv.at[0], **other(**partner))
    whole_part.wait_send()

    def finish(g, carry):
        to_copy(g).wait_recv()
        band = group(g)
        out[:, band] = qout[:, band] + qin[:, band]
        return carry

    lax.fori_loop(0, GROUPS, finish, 0)
    whole_copy = pltpu.make_async_remote_copy(
        src_ref=qout, dst_ref=qin, send_sem=qsend, recv_sem=qrecv.at[0], **other(**copy_x))
    whole_copy.wait_send()


def lent_product(left_matrix, right_matrix, layers, rows):
    height = left_matrix.shape[1]
    width = right_matrix.shape[2]
    share = left_matrix.shape[2] // layers
    f32 = jnp.float32
    dma = pltpu.SemaphoreType.DMA
    block = (2, height, width)
    return pl.pallas_call(
        functools.partial(kernel, rows),
        out_shape=jax.ShapeDtypeStruct(block, f32),
        in_specs=[pl.BlockSpec(memory_space=pl.ANY)] * 2,
        out_specs=pl.BlockSpec(memory_space=pltpu.VMEM),
        scratch_shapes=[
            pltpu.VMEM((2, 2, height, share), f32),
            pltpu.VMEM((2, 2, 2, share, width), f32),
            pltpu.VMEM((2, height, share), f32),
            pltpu.VMEM((2, height, share // CHUNKS), f32),
            pltpu.VMEM((3, height, 2 * width), f32),
            pltpu.VMEM((3, height, 2 * width), f32),
            pltpu.VMEM((2,) + block, f32),
            pltpu.VMEM(block, f32),
            pltpu.VMEM(block, f32),
            pltpu.VMEM(block, f32),
            pltpu.VMEM(block, f32),
            pltpu.VMEM(block, f32),
            dma,
            dma((3,)),
            dma((2, 2)),
            dma((2, CHUNKS * FINE)),
            dma((2,)),
            dma((2,)),
            dma((CHUNKS,)),
            dma,
            dma((CHUNKS,)),
            dma((2,)),
            dma((2,)),
            dma((GROUPS,)),
            dma,
            dma((GROUPS,)),
            dma,
            dma((GROUPS,)),
            pltpu.SemaphoreType.REGULAR,
        ],
        compiler_params=pltpu.CompilerParams(
            collective_id=0, has_side_effects=True, vmem_limit_bytes=60 * 2**20),
    )(left_matrix, right_matrix)


def gathered_product(left_matrix, right_matrix, layers):
    layer_index = lax.axis_index("layer")
    local_cols = right_matrix.shape[2]
    left_width = left_matrix.shape[2]
    right_height = right_matrix.shape[1]
    share_width = left_width // layers
    group_count = right_height // left_width
    left_own = lax.dynamic_slice_in_dim(left_matrix, layer_index * share_width, share_width, 2)
    right_view = right_matrix.reshape(2, group_count, layers, share_width, local_cols)
    right_own = lax.dynamic_slice_in_dim(right_view, layer_index, 1, 2)
    right_own = right_own.reshape(2, group_count * share_width, local_cols)
    right_whole = lax.all_gather(right_own, "row", axis=1, tiled=True)
    left_whole = lax.all_gather(left_own, "col", axis=2, tiled=True)
    dot = functools.partial(
        jnp.dot, precision=lax.Precision.HIGHEST, preferred_element_type=jnp.float32)
    first_term = dot(left_whole[0], right_whole[0])
    second_term = dot(left_whole[1], right_whole[1])
    third_term = dot(left_whole[0] + left_whole[1], right_whole[0] + right_whole[1])
    partial_product = jnp.stack([first_term - second_term, third_term - first_term - second_term])
    return lax.psum(partial_product, "layer")


def local(left_matrix, right_matrix):
    layers = lax.axis_size("layer")
    rows = lax.axis_size("row")
    cols = lax.axis_size("col")
    if layers == 2 and rows == cols == 4:
        return lent_product(left_matrix, right_matrix, layers, rows)
    return gathered_product(left_matrix, right_matrix, layers)


def solution(mesh):
    in_specs = (P(None, "row", "col"), P(None, "row", "col"))
    out_specs = P(None, "row", "col")
    return jax.shard_map(local, mesh=mesh, in_specs=in_specs, out_specs=out_specs, check_vma=False)
```

time: 118 us -> 113 us (0.958); the launches traced: 116 us -> 113 us
  Pallas kernels: 114 us -> 111 us
    pallas_call x1, Pallas kernels: 114 us -> 111 us  [lent_product(): pl.pallas_call(functools.partial(kernel, rows), out_shape=jax.ShapeDtypeS...]
where the time goes in v1:
time: 113 us
  Pallas kernels  111 us (98%)
  local copies, waits for them, and re-layouts  1.67 us (1%)
    pallas_call x1, Pallas kernels, lent_product(): pl.pallas_call(functools.partial(kernel, rows), out_shape=jax.ShapeDtypeS...  111 us

profile of v1, /device:TPU:0, one launch (start us, length us, event | category | flops | bytes accessed | tf_op | source)
XLA Modules:
  0.0 113.2 jit_solution(10330070490659677901)
XLA Ops:
  0.0 111.5 %shard_map.28 = f32[2,256,128]{2,1,0:T(8,128)} custom-call(f32[2,256,4096]{2,1,0:T(8,128)} %left.1, f32[2,4096,128]{2,1,0:T(8,128)} %right.1), custom_call_target="tpu_custom_call" | custom-call | tf_op jit(solution)/shard_map/pallas_call | solution.py:505
  111.5 1.7 %copy.4 = f32[2,256,128]{2,1,0:T(8,128)} copy(f32[2,256,128]{2,1,0:T(8,128)} %shard_map.28) | data formatting | bytes 524288

commit v2 on v1

--- a/solution.py
+++ b/solution.py
@@ -13,9 +13,9 @@
 MESH = pl.DeviceIdType.MESH
 
 
-def kernel(rows, left, right, out, abuf, bbuf, xbuf, ebuf, acc, xacc, xout, xin, pout, pin, qout, qin,
+def kernel(rows, left, right, own_out, qin, abuf, bbuf, xbuf, ebuf, acc, xacc, xout, xin, pout, pin, qout,
            own_sem, bsend, rsend, brecv, bown, ysend, yrecv, xsend, xrecv, esem, csend, crecv,
-           psend, precv, qsend, qrecv, turn):
+           psend, precv, qsend, qrecv, qsave, turn):
     x = lax.axis_index("layer")
     z = lax.axis_index("row")
     col = lax.axis_index("col")
@@ -317,6 +317,39 @@
         xacc[1, band] += dot(a_im, b_im)
         xacc[2, band] += dot(a_re + a_im, b_re + b_im)
 
+    def combined(totals, h, g):
+        first, second, third = (totals[k, group(g), half(h)] for k in range(3))
+        return first - second, third - first - second
+
+    def lend_back(h, g):
+        return pltpu.make_async_remote_copy(
+            src_ref=xout.at[h, :, group(g)], dst_ref=xin.at[:, group(g)],
+            send_sem=csend.at[h], recv_sem=crecv.at[g], **other(row=outward, col=y * 2 + h))
+
+    def lent_back(h):
+        return pltpu.make_async_remote_copy(
+            src_ref=xout.at[h], dst_ref=xin, send_sem=csend.at[h], recv_sem=crecv.at[0],
+            **other(row=outward, col=y * 2 + h))
+
+    def lent_arrival(g):
+        ref = xin.at[:, group(g)]
+        return pltpu.make_async_copy(ref, ref, crecv.at[g])
+
+    def give(g, carry):
+        for h in range(2):
+            xout[h, 0, group(g)], xout[h, 1, group(g)] = combined(xacc, h, g)
+        for h in range(2):
+            lend_back(h, g).start()
+        return carry
+
+    def extra_multiply():
+        e_own.wait_recv()
+        b_re, b_im = both(1 - z // 2, span(tail))
+        xacc[0] += dot(ebuf[0], b_re)
+        xacc[1] += dot(ebuf[1], b_im)
+        xacc[2] += dot(ebuf[0] + ebuf[1], b_re + b_im)
+        lax.fori_loop(0, GROUPS - 1, give, 0)
+
     def right_step(i):
         for s in range(2):
             @pl.when(present(s) & jnp.logical_not(is_own(s)) & jnp.logical_not(at_end & is_far(s) & (i == tail)))
@@ -329,6 +362,10 @@
                         relay(s, i * FINE + k, (i == tail).astype(jnp.int32),
                               jnp.where(goes_up(s), z + 1, z - 1)).start()
 
+        @pl.when(helps & (i == tail))
+        def _():
+            extra_multiply()
+
         @pl.when(present(y))
         def _():
             multiply(abuf.at[y], y, i)
@@ -351,6 +388,10 @@
         def _():
             x_arrival(i).wait()
             lent_multiply(i)
+
+            @pl.when(i == tail)
+            def _():
+                give(GROUPS - 1, 0)
 
     early = jnp.logical_not(at_end) & (c != parity)
 
@@ -373,44 +414,6 @@
 
     lax.fori_loop(0, 2 * CHUNKS, work, 0)
 
-    def combined(totals, h, g):
-        first, second, third = (totals[k, group(g), half(h)] for k in range(3))
-        return first - second, third - first - second
-
-    def lend_back(h, g):
-        return pltpu.make_async_remote_copy(
-            src_ref=xout.at[h, :, group(g)], dst_ref=xin.at[:, group(g)],
-            send_sem=csend.at[h], recv_sem=crecv.at[g], **other(row=outward, col=y * 2 + h))
-
-    def lent_back(h):
-        return pltpu.make_async_remote_copy(
-            src_ref=xout.at[h], dst_ref=xin, send_sem=csend.at[h], recv_sem=crecv.at[0],
-            **other(row=outward, col=y * 2 + h))
-
-    def lent_arrival(g):
-        ref = xin.at[:, group(g)]
-        return pltpu.make_async_copy(ref, ref, crecv.at[g])
-
-    @pl.when(helps)
-    def _():
-        e_own.wait_recv()
-        at = span(tail)
-
-        def give(g, carry):
-            band = group(g)
-            a_re, a_im = ebuf[0, band, :], ebuf[1, band, :]
-            b_re, b_im = both(1 - z // 2, at)
-            xacc[0, band] += dot(a_re, b_re)
-            xacc[1, band] += dot(a_im, b_im)
-            xacc[2, band] += dot(a_re + a_im, b_re + b_im)
-            for h in range(2):
-                xout[h, 0, band], xout[h, 1, band] = combined(xacc, h, g)
-            for h in range(2):
-                lend_back(h, g).start()
-            return carry
-
-        lax.fori_loop(0, GROUPS, give, 0)
-
     def to_partner(g):
         return pltpu.make_async_remote_copy(
             src_ref=pout.at[:, group(g)], dst_ref=pin.at[:, group(g)],
@@ -419,7 +422,10 @@
     def to_copy(g):
         return pltpu.make_async_remote_copy(
             src_ref=qout.at[:, group(g)], dst_ref=qin.at[:, group(g)],
-            send_sem=qsend, recv_sem=qrecv.at[g], **other(**copy_x))
+            send_sem=qsend, recv_sem=qrecv, **other(**copy_x))
+
+    def keep(g):
+        return pltpu.make_async_copy(qout.at[:, group(g)], own_out.at[:, group(g)], qsave)
 
     def hand(g, carry):
         pout[0, group(g)], pout[1, group(g)] = combined(acc, 1 - c, g)
@@ -441,6 +447,7 @@
             qout[:, band] += xin[:, band]
 
         to_copy(g).start()
+        keep(g).start()
         return carry
 
     lax.fori_loop(0, GROUPS, gather, 0)
@@ -483,16 +490,10 @@
         src_ref=pout, dst_ref=pin, send_sem=psend, recv_sem=precv.at[0], **other(**partner))
     whole_part.wait_send()
 
-    def finish(g, carry):
-        to_copy(g).wait_recv()
-        band = group(g)
-        out[:, band] = qout[:, band] + qin[:, band]
-        return carry
-
-    lax.fori_loop(0, GROUPS, finish, 0)
+    pltpu.make_async_copy(qout, own_out, qsave).wait()
     whole_copy = pltpu.make_async_remote_copy(
-        src_ref=qout, dst_ref=qin, send_sem=qsend, recv_sem=qrecv.at[0], **other(**copy_x))
-    whole_copy.wait_send()
+        src_ref=qout, dst_ref=qin, send_sem=qsend, recv_sem=qrecv, **other(**copy_x))
+    whole_copy.wait()
 
 
 def lent_product(left_matrix, right_matrix, layers, rows):
@@ -502,11 +503,11 @@
     f32 = jnp.float32
     dma = pltpu.SemaphoreType.DMA
     block = (2, height, width)
-    return pl.pallas_call(
+    own, copied = pl.pallas_call(
         functools.partial(kernel, rows),
-        out_shape=jax.ShapeDtypeStruct(block, f32),
+        out_shape=[jax.ShapeDtypeStruct(block, f32)] * 2,
         in_specs=[pl.BlockSpec(memory_space=pl.ANY)] * 2,
-        out_specs=pl.BlockSpec(memory_space=pltpu.VMEM),
+        out_specs=[pl.BlockSpec(memory_space=pl.ANY)] * 2,
         scratch_shapes=[
             pltpu.VMEM((2, 2, height, share), f32),
             pltpu.VMEM((2, 2, 2, share, width), f32),
@@ -515,7 +516,6 @@
             pltpu.VMEM((3, height, 2 * width), f32),
             pltpu.VMEM((3, height, 2 * width), f32),
             pltpu.VMEM((2,) + block, f32),
-            pltpu.VMEM(block, f32),
             pltpu.VMEM(block, f32),
             pltpu.VMEM(block, f32),
             pltpu.VMEM(block, f32),
@@ -535,12 +535,14 @@
             dma,
             dma((GROUPS,)),
             dma,
-            dma((GROUPS,)),
+            dma,
+            dma,
             pltpu.SemaphoreType.REGULAR,
         ],
         compiler_params=pltpu.CompilerParams(
             collective_id=0, has_side_effects=True, vmem_limit_bytes=60 * 2**20),
     )(left_matrix, right_matrix)
+    return own + copied
 
 
 def gathered_product(left_matrix, right_matrix, layers):

time: 113 us -> 111 us (0.982)
  Pallas kernels: 111 us -> 109 us
  other arithmetic: 0 us -> 1.76 us
  local copies, waits for them, and re-layouts: 1.67 us -> 0 us
    pallas_call x1, Pallas kernels: 111 us -> 109 us  [lent_product(): pl.pallas_call(functools.partial(kernel, rows), out_shape=[jax.ShapeDtype...]
    add x0 -> x1, other arithmetic: none -> 1.76 us  [lent_product(): return own + copied]
    unnamed x1 -> x0, local copies, waits for them, and re-layouts: 1.67 us -> none
where the time goes in v2:
time: 111 us
  Pallas kernels  109 us (98%)
  other arithmetic  1.76 us (2%)
    pallas_call x1, Pallas kernels, lent_product(): pl.pallas_call(functools.partial(kernel, rows), out_shape=[jax.ShapeDtype...  109 us

profile of v2, /device:TPU:0, one launch (start us, length us, event | category | flops | bytes accessed | tf_op | source)
XLA Modules:
  0.0 110.7 jit_solution(14916566916953744224)
XLA Ops:
  0.0 108.9 %shard_map.28 = (f32[2,256,128]{2,1,0:T(8,128)}, f32[2,256,128]{2,1,0:T(8,128)}) custom-call(f32[2,256,4096]{2,1,0:T(8,128)} %left.1, f32[2,4096,128]{2,1,0:T(8,128)} %right.1), custom_call_target="tpu_custom_call" | custom-call | tf_op jit(solution)/shard_map/pallas_call | solution.py:506
  108.9 1.8 %add.3 = f32[2,256,128]{2,1,0:T(8,128)} add(f32[2,256,128]{2,1,0:T(8,128)} %get-tuple-element.7, f32[2,256,128]{2,1,0:T(8,128)} %get-tuple-element.8) | non-fusion elementwise | flops 65536 | bytes 786432 | tf_op jit(solution)/shard_map/add | solution.py:545

commit v3 on v2

--- a/solution.py
+++ b/solution.py
@@ -10,12 +10,14 @@
 CHUNKS = 16
 FINE = 2
 GROUPS = 4
+LAG = 2
+BANDS = 8
 MESH = pl.DeviceIdType.MESH
 
 
-def kernel(rows, left, right, own_out, qin, abuf, bbuf, xbuf, ebuf, acc, xacc, xout, xin, pout, pin, qout,
+def kernel(rows, left, right, qout, qin, abuf, bbuf, xbuf, ebuf, acc, xacc, xout, xin, pout, pin,
            own_sem, bsend, rsend, brecv, bown, ysend, yrecv, xsend, xrecv, esem, csend, crecv,
-           psend, precv, qsend, qrecv, qsave, turn):
+           psend, precv, qsend, qrecv, turn):
     x = lax.axis_index("layer")
     z = lax.axis_index("row")
     col = lax.axis_index("col")
@@ -370,6 +372,10 @@
         def _():
             multiply(abuf.at[y], y, i)
 
+    def lent_step(i):
+        x_arrival(i).wait()
+        lent_multiply(i)
+
     def left_step(i):
         @pl.when(jnp.logical_not(lends_relayed | (lends_own & (i == tail))))
         def _():
@@ -384,14 +390,9 @@
         def _():
             multiply(abuf.at[1 - y], 1 - y, i)
 
-        @pl.when(helps)
-        def _():
-            x_arrival(i).wait()
-            lent_multiply(i)
-
-            @pl.when(i == tail)
-            def _():
-                give(GROUPS - 1, 0)
+        @pl.when(helps & (i >= LAG))
+        def _():
+            lent_step(i - LAG)
 
     early = jnp.logical_not(at_end) & (c != parity)
 
@@ -414,43 +415,58 @@
 
     lax.fori_loop(0, 2 * CHUNKS, work, 0)
 
-    def to_partner(g):
-        return pltpu.make_async_remote_copy(
-            src_ref=pout.at[:, group(g)], dst_ref=pin.at[:, group(g)],
-            send_sem=psend, recv_sem=precv.at[g], **other(**partner))
-
-    def to_copy(g):
-        return pltpu.make_async_remote_copy(
-            src_ref=qout.at[:, group(g)], dst_ref=qin.at[:, group(g)],
+    @pl.when(helps)
+    def _():
+        def lent_rest(i, carry):
+            lent_step(i)
+            return carry
+        lax.fori_loop(CHUNKS - LAG, CHUNKS, lent_rest, 0)
+        give(GROUPS - 1, 0)
+
+    thin = height // BANDS
+
+    def band_of(b):
+        return pl.ds(pl.multiple_of(b * thin, thin), thin)
+
+    def banded(h, b):
+        first, second, third = (acc[k, band_of(b), half(h)] for k in range(3))
+        return first - second, third - first - second
+
+    def to_partner(b):
+        return pltpu.make_async_remote_copy(
+            src_ref=pout.at[:, band_of(b)], dst_ref=pin.at[:, band_of(b)],
+            send_sem=psend, recv_sem=precv.at[b], **other(**partner))
+
+    def to_copy(b):
+        return pltpu.make_async_remote_copy(
+            src_ref=qout.at[:, band_of(b)], dst_ref=qin.at[:, band_of(b)],
             send_sem=qsend, recv_sem=qrecv, **other(**copy_x))
 
-    def keep(g):
-        return pltpu.make_async_copy(qout.at[:, group(g)], own_out.at[:, group(g)], qsave)
-
-    def hand(g, carry):
-        pout[0, group(g)], pout[1, group(g)] = combined(acc, 1 - c, g)
-        to_partner(g).start()
+    def hand(b, carry):
+        pout[0, band_of(b)], pout[1, band_of(b)] = banded(1 - c, b)
+        to_partner(b).start()
         return carry
 
-    lax.fori_loop(0, GROUPS, hand, 0)
-
-    def gather(g, carry):
-        band = group(g)
-        mine_re, mine_im = combined(acc, c, g)
-        to_partner(g).wait_recv()
+    lax.fori_loop(0, BANDS, hand, 0)
+
+    def gather(b, carry):
+        band = band_of(b)
+        mine_re, mine_im = banded(c, b)
+        to_partner(b).wait_recv()
         qout[0, band] = mine_re + pin[0, band]
         qout[1, band] = mine_im + pin[1, band]
 
         @pl.when(at_end)
         def _():
-            lent_arrival(g).wait()
+            @pl.when(b % (BANDS // GROUPS) == 0)
+            def _():
+                lent_arrival(b // (BANDS // GROUPS)).wait()
             qout[:, band] += xin[:, band]
 
-        to_copy(g).start()
-        keep(g).start()
+        to_copy(b).start()
         return carry
 
-    lax.fori_loop(0, GROUPS, gather, 0)
+    lax.fori_loop(0, BANDS, gather, 0)
 
     @pl.when(sends_up)
     def _():
@@ -490,7 +506,6 @@
         src_ref=pout, dst_ref=pin, send_sem=psend, recv_sem=precv.at[0], **other(**partner))
     whole_part.wait_send()
 
-    pltpu.make_async_copy(qout, own_out, qsave).wait()
     whole_copy = pltpu.make_async_remote_copy(
         src_ref=qout, dst_ref=qin, send_sem=qsend, recv_sem=qrecv, **other(**copy_x))
     whole_copy.wait()
@@ -505,9 +520,9 @@
     block = (2, height, width)
     own, copied = pl.pallas_call(
         functools.partial(kernel, rows),
-        out_shape=[jax.ShapeDtypeStruct(block, f32)] * 2,
+        out_shape=[pltpu.VMEM(block, f32)] * 2,
         in_specs=[pl.BlockSpec(memory_space=pl.ANY)] * 2,
-        out_specs=[pl.BlockSpec(memory_space=pl.ANY)] * 2,
+        out_specs=[pl.BlockSpec(memory_space=pltpu.VMEM)] * 2,
         scratch_shapes=[
             pltpu.VMEM((2, 2, height, share), f32),
             pltpu.VMEM((2, 2, 2, share, width), f32),
@@ -516,7 +531,6 @@
             pltpu.VMEM((3, height, 2 * width), f32),
             pltpu.VMEM((3, height, 2 * width), f32),
             pltpu.VMEM((2,) + block, f32),
-            pltpu.VMEM(block, f32),
             pltpu.VMEM(block, f32),
             pltpu.VMEM(block, f32),
             pltpu.VMEM(block, f32),
@@ -533,8 +547,7 @@
             dma((2,)),
             dma((GROUPS,)),
             dma,
-            dma((GROUPS,)),
-            dma,
+            dma((BANDS,)),
             dma,
             dma,
             pltpu.SemaphoreType.REGULAR,

time: 111 us -> 110 us (level)
  no operation moved by 1% of the time
where the time goes in v3:
time: 110 us
  Pallas kernels  109 us (99%)
    pallas_call x1, Pallas kernels, lent_product(): pl.pallas_call(functools.partial(kernel, rows), out_shape=[pltpu.VMEM(blo...  109 us

profile of v3, /device:TPU:0, one launch (start us, length us, event | category | flops | bytes accessed | tf_op | source)
XLA Modules:
  0.0 109.7 jit_solution(5206736566745891348)
XLA Ops:
  0.0 108.9 %shard_map.28 = (f32[2,256,128]{2,1,0:T(8,128)S(1)}, f32[2,256,128]{2,1,0:T(8,128)S(1)}) custom-call(f32[2,256,4096]{2,1,0:T(8,128)} %left.1, f32[2,4096,128]{2,1,0:T(8,128)} %right.1), custom_call_target="tpu_custom_call" | custom-call | tf_op jit(solution)/shard_map/pallas_call | solution.py:521
  108.9 0.7 add.3

commit v4 on v3

--- a/solution.py
+++ b/solution.py
@@ -10,7 +10,9 @@
 CHUNKS = 16
 FINE = 2
 GROUPS = 4
-LAG = 2
+EXTRA = 2
+FILL = 2
+LAG = 1
 BANDS = 8
 MESH = pl.DeviceIdType.MESH
 
@@ -29,9 +31,12 @@
     step = share // CHUNKS
     fine = step // FINE
     tall = height // GROUPS
-    wide = share // GROUPS
+    parts = CHUNKS // GROUPS
+    wide = share // parts
+    fill = FILL * step
     last = rows - 1
     tail = CHUNKS - 1
+    kept = CHUNKS - EXTRA
     base = x * share
     parity = z % 2
     at_low, at_high = z == 0, z == last
@@ -87,17 +92,23 @@
     def half(h):
         return pl.ds(pl.multiple_of(h * width, width), width)
 
+    thin = height // BANDS
+    per = BANDS // GROUPS
+
+    def band_of(b):
+        return pl.ds(pl.multiple_of(b * thin, thin), thin)
+
     def group(g):
         return pl.ds(pl.multiple_of(g * tall, tall), tall)
 
     def piece_rows(i):
-        return group(i // GROUPS)
+        return group(i // parts)
 
     def piece_cols(i):
-        return pl.ds(pl.multiple_of((i % GROUPS) * wide, wide), wide)
+        return pl.ds(pl.multiple_of((i % parts) * wide, wide), wide)
 
     def piece_source(i):
-        return pl.ds(pl.multiple_of(base + (i % GROUPS) * wide, step), wide)
+        return pl.ds(pl.multiple_of(base + (i % parts) * wide, step), wide)
 
     whole_source = pl.ds(pl.multiple_of(base, step), share)
 
@@ -130,6 +141,12 @@
             dst_ref=abuf.at[y, :, piece_rows(i), piece_cols(i)],
             send_sem=ysend.at[y_part(i)], recv_sem=yrecv.at[i], **other(**across))
 
+    def late(i):
+        return i >= kept
+
+    late_span = pl.ds(kept * step, EXTRA * step)
+    late_source = pl.ds(pl.multiple_of(base + kept * step, step), EXTRA * step)
+
     def y_sent(part):
         size = (tail if part == 0 else 1) * step
         ref = abuf.at[y, :, :, pl.ds(0, size)]
@@ -144,38 +161,59 @@
         ref = abuf.at[1 - y, :, piece_rows(i), piece_cols(i)]
         return pltpu.make_async_copy(ref, ref, yrecv.at[i])
 
+    def by_piece(i, act):
+        @pl.when(i % parts == 0)
+        def _():
+            act(piece_rows(i), fill, pl.multiple_of(base + fill, step), wide - fill)
+
+        @pl.when(i % parts != 0)
+        def _():
+            start = pl.multiple_of((i % parts) * wide, wide)
+            act(piece_rows(i), start, pl.multiple_of(base + start, step), wide)
+
     def x_own(i):
-        return pltpu.make_async_remote_copy(
-            src_ref=left.at[:, piece_rows(i), piece_source(i)],
-            dst_ref=xbuf.at[:, piece_rows(i), piece_cols(i)],
-            send_sem=xsend, recv_sem=xrecv.at[i], **other(row=inward))
+        def act(band, start, source, size):
+            pltpu.make_async_remote_copy(
+                src_ref=left.at[:, band, pl.ds(source, size)],
+                dst_ref=xbuf.at[:, band, pl.ds(start, size)],
+                send_sem=xsend, recv_sem=xrecv.at[i], **other(row=inward)).start()
+        by_piece(i, act)
 
     def x_relay(i):
-        return pltpu.make_async_remote_copy(
-            src_ref=abuf.at[1 - y, :, piece_rows(i), piece_cols(i)],
-            dst_ref=xbuf.at[:, piece_rows(i), piece_cols(i)],
-            send_sem=xsend, recv_sem=xrecv.at[i], **other(row=inward))
-
-    def x_arrival(i):
-        ref = xbuf.at[:, piece_rows(i), piece_cols(i)]
-        return pltpu.make_async_copy(ref, ref, xrecv.at[i])
-
+        def act(band, start, source, size):
+            pltpu.make_async_remote_copy(
+                src_ref=abuf.at[1 - y, :, band, pl.ds(start, size)],
+                dst_ref=xbuf.at[:, band, pl.ds(start, size)],
+                send_sem=xsend, recv_sem=xrecv.at[i], **other(row=inward)).start()
+        by_piece(i, act)
+
+    lent_ref = xbuf.at[:, :, pl.ds(fill, share - fill)]
     x_sent = pltpu.make_async_remote_copy(
-        src_ref=xbuf, dst_ref=xbuf, send_sem=xsend, recv_sem=xrecv.at[0], **other(row=inward))
+        src_ref=lent_ref, dst_ref=lent_ref, send_sem=xsend, recv_sem=xrecv.at[0], **other(row=inward))
     e_own = pltpu.make_async_remote_copy(
-        src_ref=left.at[:, :, source_span(tail)], dst_ref=ebuf,
+        src_ref=left.at[:, :, late_source], dst_ref=ebuf,
         send_sem=esem.at[0], recv_sem=esem.at[1], **other(row=inward))
     e_relay = pltpu.make_async_remote_copy(
-        src_ref=abuf.at[1 - y, :, :, span(tail)], dst_ref=ebuf,
+        src_ref=abuf.at[1 - y, :, :, late_span], dst_ref=ebuf,
         send_sem=esem.at[0], recv_sem=esem.at[1], **other(row=inward))
 
     yields = at_end & jnp.logical_not(lends) & (y == lent_slot)
     sends_up = (z < last) & (z != last - 1)
     sends_down = (z > 0) & (z != 1)
 
+    fills_down = z == 1
+    fills_up = z == last - 1
+    fill_row = jnp.where(fills_down, 0, last)
+
+    @pl.when(fills_down | fills_up)
+    def _():
+        for u in range(FILL * FINE):
+            b_copy(u, 3, fill_row).start()
+
     @pl.when(lends_relayed)
     def _():
-        y_copy(tail).start()
+        for i in range(kept, CHUNKS):
+            y_copy(i).start()
 
     def launch(i, carry):
         for k in range(FINE):
@@ -187,7 +225,7 @@
             def _():
                 b_copy(i * FINE + k, 1, z - 1).start()
 
-        @pl.when(jnp.logical_not(yields | lends_own) & jnp.logical_not(lends_relayed & (i == tail)))
+        @pl.when(jnp.logical_not(yields | lends_own) & jnp.logical_not(lends_relayed & late(i)))
         def _():
             y_copy(i).start()
 
@@ -213,11 +251,12 @@
 
     @pl.when(lends_own)
     def _():
-        y_arrival(tail).wait()
+        for i in range(kept, CHUNKS):
+            y_arrival(i).wait()
         e_relay.start()
 
         def lend(i, carry):
-            x_own(i).start()
+            x_own(i)
             return carry
         lax.fori_loop(0, CHUNKS, lend, 0)
         y_sent(0).wait_send()
@@ -250,7 +289,7 @@
             **other(row=row))
 
     def relayed(s, part):
-        start, size = ((0, tail) if part == 0 else (tail, 1))
+        start, size = ((0, kept) if part == 0 else (kept, EXTRA))
         ref = bbuf.at[s, :, :, pl.ds(start * step, size * step), :]
         return pltpu.make_async_remote_copy(
             src_ref=ref, dst_ref=ref, send_sem=rsend.at[s, part], recv_sem=brecv.at[s, 0],
@@ -275,7 +314,7 @@
         return (quarter > z) & (z > 0)
 
     def goes(s, i):
-        cut = is_far(s) & ((z == 1) | (z == last - 1)) & (i == tail)
+        cut = is_far(s) & ((z == 1) | (z == last - 1)) & late(i)
         return (goes_up(s) | goes_down(s)) & jnp.logical_not(cut)
 
     def split(value):
@@ -293,98 +332,116 @@
     def both(s, at):
         return (jnp.concatenate([bbuf[s, h, k, at, :] for h in range(2)], axis=1) for k in range(2))
 
+    def accumulate(a_ref, s, at):
+        a_re, a_im = a_ref[0, :, at], a_ref[1, :, at]
+        b_re, b_im = both(s, at)
+        acc[0] += dot(a_re, b_re)
+        acc[1] += dot(a_im, b_im)
+        acc[2] += dot(a_re + a_im, b_re + b_im)
+
     def multiply(a_ref, s, i):
-        def add(at):
-            a_re, a_im = a_ref[0, :, at], a_ref[1, :, at]
-            b_re, b_im = both(s, at)
-            acc[0] += dot(a_re, b_re)
-            acc[1] += dot(a_im, b_im)
-            acc[2] += dot(a_re + a_im, b_re + b_im)
-
-        alone = at_end & is_far(s) & (i == tail)
-
-        @pl.when((i % 2 == 1) & jnp.logical_not(alone))
-        def _():
-            add(pl.ds(pl.multiple_of((i - 1) * step, 2 * step), 2 * step))
-
-        @pl.when(alone)
-        def _():
-            add(span(i - 1))
-
-    def lent_multiply(i):
-        at, band = piece_cols(i), piece_rows(i)
-        a_re, a_im = xbuf[0, band, at], xbuf[1, band, at]
-        b_re, b_im = both(z // 2, at)
-        xacc[0, band] += dot(a_re, b_re)
-        xacc[1, band] += dot(a_im, b_im)
-        xacc[2, band] += dot(a_re + a_im, b_re + b_im)
+
+        @pl.when((i % 2 == 1) & jnp.logical_not(at_end & is_far(s) & late(i)))
+        def _():
+            accumulate(a_ref, s, pl.ds(pl.multiple_of((i - 1) * step, 2 * step), 2 * step))
+
+    def lent_step(i):
+        def act(band, start, source, size):
+            ref = xbuf.at[:, band, pl.ds(start, size)]
+            pltpu.make_async_copy(ref, ref, xrecv.at[i]).wait()
+            at = pl.ds(start, size)
+            a_re, a_im = xbuf[0, band, at], xbuf[1, band, at]
+            b_re, b_im = both(z // 2, at)
+            xacc[0, band] += dot(a_re, b_re)
+            xacc[1, band] += dot(a_im, b_im)
+            xacc[2, band] += dot(a_re + a_im, b_re + b_im)
+        by_piece(i, act)
 
     def combined(totals, h, g):
         first, second, third = (totals[k, group(g), half(h)] for k in range(3))
         return first - second, third - first - second
 
-    def lend_back(h, g):
-        return pltpu.make_async_remote_copy(
-            src_ref=xout.at[h, :, group(g)], dst_ref=xin.at[:, group(g)],
-            send_sem=csend.at[h], recv_sem=crecv.at[g], **other(row=outward, col=y * 2 + h))
+    def lend_back(h, b):
+        return pltpu.make_async_remote_copy(
+            src_ref=xout.at[h, :, band_of(b)], dst_ref=xin.at[:, band_of(b)],
+            send_sem=csend.at[h], recv_sem=crecv.at[b], **other(row=outward, col=y * 2 + h))
 
     def lent_back(h):
         return pltpu.make_async_remote_copy(
             src_ref=xout.at[h], dst_ref=xin, send_sem=csend.at[h], recv_sem=crecv.at[0],
             **other(row=outward, col=y * 2 + h))
 
-    def lent_arrival(g):
-        ref = xin.at[:, group(g)]
-        return pltpu.make_async_copy(ref, ref, crecv.at[g])
-
-    def give(g, carry):
+    def lent_arrival(b):
+        ref = xin.at[:, band_of(b)]
+        return pltpu.make_async_copy(ref, ref, crecv.at[b])
+
+    def give(g):
         for h in range(2):
             xout[h, 0, group(g)], xout[h, 1, group(g)] = combined(xacc, h, g)
-        for h in range(2):
-            lend_back(h, g).start()
-        return carry
-
-    def extra_multiply():
-        e_own.wait_recv()
-        b_re, b_im = both(1 - z // 2, span(tail))
-        xacc[0] += dot(ebuf[0], b_re)
-        xacc[1] += dot(ebuf[1], b_im)
-        xacc[2] += dot(ebuf[0] + ebuf[1], b_re + b_im)
-        lax.fori_loop(0, GROUPS - 1, give, 0)
+        for k in range(per):
+            for h in range(2):
+                lend_back(h, g * per + k).start()
+
+    def extra_step(i):
+        @pl.when(i == kept)
+        def _():
+            e_own.wait_recv()
+
+        b_re, b_im = both(1 - z // 2, span(i))
+        b_sum = b_re + b_im
+        at = span(i - kept)
+
+        def add(g):
+            band = group(g)
+            a_re, a_im = ebuf[0, band, at], ebuf[1, band, at]
+            xacc[0, band] += dot(a_re, b_re)
+            xacc[1, band] += dot(a_im, b_im)
+            xacc[2, band] += dot(a_re + a_im, b_sum)
+
+        for g in range(GROUPS):
+            add(g)
+            if g < GROUPS - 1:
+                @pl.when(i == tail)
+                def _():
+                    give(g)
 
     def right_step(i):
-        for s in range(2):
-            @pl.when(present(s) & jnp.logical_not(is_own(s)) & jnp.logical_not(at_end & is_far(s) & (i == tail)))
+        for n in range(2):
+            s = jnp.where(z < rows // 2, 1 - n, n)
+
+            @pl.when(present(s) & jnp.logical_not(is_own(s)) & jnp.logical_not(at_end & is_far(s) & late(i)))
             def _():
                 for k in range(FINE):
                     b_arrival(s, i * FINE + k).wait()
 
                     @pl.when(goes(s, i))
                     def _():
-                        relay(s, i * FINE + k, (i == tail).astype(jnp.int32),
+                        relay(s, i * FINE + k, late(i).astype(jnp.int32),
                               jnp.where(goes_up(s), z + 1, z - 1)).start()
 
-        @pl.when(helps & (i == tail))
-        def _():
-            extra_multiply()
+        @pl.when(helps & late(i))
+        def _():
+            extra_step(i)
+
+        @pl.when(lends & (i == 0))
+        def _():
+            for u in range(FILL * FINE):
+                b_arrival(lent_slot, u).wait()
+            accumulate(abuf.at[lent_slot], lent_slot, pl.ds(0, fill))
 
         @pl.when(present(y))
         def _():
             multiply(abuf.at[y], y, i)
 
-    def lent_step(i):
-        x_arrival(i).wait()
-        lent_multiply(i)
-
     def left_step(i):
-        @pl.when(jnp.logical_not(lends_relayed | (lends_own & (i == tail))))
+        @pl.when(jnp.logical_not(lends_relayed | (lends_own & late(i))))
         def _():
             y_arrival(i).wait()
 
         @pl.when(lends_relayed)
         def _():
             y_piece_arrival(i).wait()
-            x_relay(i).start()
+            x_relay(i)
 
         @pl.when(present(1 - y))
         def _():
@@ -415,39 +472,34 @@
 
     lax.fori_loop(0, 2 * CHUNKS, work, 0)
 
+    def banded(h, b):
+        first, second, third = (acc[k, band_of(b), half(h)] for k in range(3))
+        return first - second, third - first - second
+
+    def to_partner(b):
+        return pltpu.make_async_remote_copy(
+            src_ref=pout.at[:, band_of(b)], dst_ref=pin.at[:, band_of(b)],
+            send_sem=psend, recv_sem=precv.at[b], **other(**partner))
+
+    def to_copy(b):
+        return pltpu.make_async_remote_copy(
+            src_ref=qout.at[:, band_of(b)], dst_ref=qin.at[:, band_of(b)],
+            send_sem=qsend, recv_sem=qrecv, **other(**copy_x))
+
+    def hand(b, carry):
+        pout[0, band_of(b)], pout[1, band_of(b)] = banded(1 - c, b)
+        to_partner(b).start()
+        return carry
+
+    lax.fori_loop(0, BANDS, hand, 0)
+
     @pl.when(helps)
     def _():
         def lent_rest(i, carry):
             lent_step(i)
             return carry
         lax.fori_loop(CHUNKS - LAG, CHUNKS, lent_rest, 0)
-        give(GROUPS - 1, 0)
-
-    thin = height // BANDS
-
-    def band_of(b):
-        return pl.ds(pl.multiple_of(b * thin, thin), thin)
-
-    def banded(h, b):
-        first, second, third = (acc[k, band_of(b), half(h)] for k in range(3))
-        return first - second, third - first - second
-
-    def to_partner(b):
-        return pltpu.make_async_remote_copy(
-            src_ref=pout.at[:, band_of(b)], dst_ref=pin.at[:, band_of(b)],
-            send_sem=psend, recv_sem=precv.at[b], **other(**partner))
-
-    def to_copy(b):
-        return pltpu.make_async_remote_copy(
-            src_ref=qout.at[:, band_of(b)], dst_ref=qin.at[:, band_of(b)],
-            send_sem=qsend, recv_sem=qrecv, **other(**copy_x))
-
-    def hand(b, carry):
-        pout[0, band_of(b)], pout[1, band_of(b)] = banded(1 - c, b)
-        to_partner(b).start()
-        return carry
-
-    lax.fori_loop(0, BANDS, hand, 0)
+        give(GROUPS - 1)
 
     def gather(b, carry):
         band = band_of(b)
@@ -458,9 +510,7 @@
 
         @pl.when(at_end)
         def _():
-            @pl.when(b % (BANDS // GROUPS) == 0)
-            def _():
-                lent_arrival(b // (BANDS // GROUPS)).wait()
+            lent_arrival(b).wait()
             qout[:, band] += xin[:, band]
 
         to_copy(b).start()
@@ -479,6 +529,13 @@
     @pl.when(c != parity)
     def _():
         b_partner.wait_send()
+
+    @pl.when(fills_down | fills_up)
+    def _():
+        ref = bbuf.at[z // 2, c, :, pl.ds(0, fill), :]
+        pltpu.make_async_remote_copy(
+            src_ref=ref, dst_ref=ref, send_sem=bsend.at[3], recv_sem=bown.at[1],
+            **other(**partner)).wait_send()
 
     @pl.when(jnp.logical_not(lends_own))
     def _():
@@ -527,7 +584,7 @@
             pltpu.VMEM((2, 2, height, share), f32),
             pltpu.VMEM((2, 2, 2, share, width), f32),
             pltpu.VMEM((2, height, share), f32),
-            pltpu.VMEM((2, height, share // CHUNKS), f32),
+            pltpu.VMEM((2, height, EXTRA * share // CHUNKS), f32),
             pltpu.VMEM((3, height, 2 * width), f32),
             pltpu.VMEM((3, height, 2 * width), f32),
             pltpu.VMEM((2,) + block, f32),
@@ -535,7 +592,7 @@
             pltpu.VMEM(block, f32),
             pltpu.VMEM(block, f32),
             dma,
-            dma((3,)),
+            dma((4,)),
             dma((2, 2)),
             dma((2, CHUNKS * FINE)),
             dma((2,)),
@@ -545,7 +602,7 @@
             dma((CHUNKS,)),
             dma((2,)),
             dma((2,)),
-            dma((GROUPS,)),
+            dma((BANDS,)),
             dma,
             dma((BANDS,)),
             dma,

time: 110 us -> 109 us (level)
  no operation moved by 1% of the time
where the time goes in v4:
time: 109 us
  Pallas kernels  108 us (99%)
    pallas_call x1, Pallas kernels, lent_product(): pl.pallas_call(functools.partial(kernel, rows), out_shape=[pltpu.VMEM(blo...  108 us

profile of v4, /device:TPU:0, one launch (start us, length us, event | category | flops | bytes accessed | tf_op | source)
XLA Modules:
  0.0 109.1 jit_solution(320863488430262920)
XLA Ops:
  0.0 108.4 %shard_map.28 = (f32[2,256,128]{2,1,0:T(8,128)S(1)}, f32[2,256,128]{2,1,0:T(8,128)S(1)}) custom-call(f32[2,256,4096]{2,1,0:T(8,128)} %left.1, f32[2,4096,128]{2,1,0:T(8,128)} %right.1), custom_call_target="tpu_custom_call" | custom-call | tf_op jit(solution)/shard_map/pallas_call | solution.py:578
  108.4 0.7 add.3

commit v5 on v4

--- a/solution.py
+++ b/solution.py
@@ -288,6 +288,12 @@
             src_ref=ref, dst_ref=ref, send_sem=rsend.at[s, part], recv_sem=brecv.at[s, u],
             **other(row=row))
 
+    def half_relay(s, h, row):
+        ref = bbuf.at[s, h, :, late_span, :]
+        return pltpu.make_async_remote_copy(
+            src_ref=ref, dst_ref=ref, send_sem=rsend.at[s, 1],
+            recv_sem=brecv.at[s, kept * FINE + h], **other(row=row))
+
     def relayed(s, part):
         start, size = ((0, kept) if part == 0 else (kept, EXTRA))
         ref = bbuf.at[s, :, :, pl.ds(start * step, size * step), :]
@@ -301,6 +307,10 @@
 
     def is_own(s):
         return 2 * s + c == z
+
+    def is_outer(s):
+        outer = jnp.where(z < rows // 2, 0, last)
+        return (2 * s + c == outer) & jnp.logical_not(at_end)
 
     def is_far(s):
         return 2 * s + c == far
@@ -375,53 +385,66 @@
         ref = xin.at[:, band_of(b)]
         return pltpu.make_async_copy(ref, ref, crecv.at[b])
 
-    def give(g):
-        for h in range(2):
-            xout[h, 0, group(g)], xout[h, 1, group(g)] = combined(xacc, h, g)
+    def give(h, g):
+        xout[h, 0, group(g)], xout[h, 1, group(g)] = combined(xacc, h, g)
         for k in range(per):
-            for h in range(2):
-                lend_back(h, g * per + k).start()
-
-    def extra_step(i):
-        @pl.when(i == kept)
-        def _():
+            lend_back(h, g * per + k).start()
+
+    def extra_step(h):
+        if h == 0:
             e_own.wait_recv()
 
-        b_re, b_im = both(1 - z // 2, span(i))
+        b_re, b_im = (bbuf[1 - z // 2, h, k, late_span, :] for k in range(2))
         b_sum = b_re + b_im
-        at = span(i - kept)
-
-        def add(g):
+        lanes = half(h)
+
+        for g in range(GROUPS):
             band = group(g)
-            a_re, a_im = ebuf[0, band, at], ebuf[1, band, at]
-            xacc[0, band] += dot(a_re, b_re)
-            xacc[1, band] += dot(a_im, b_im)
-            xacc[2, band] += dot(a_re + a_im, b_sum)
-
-        for g in range(GROUPS):
-            add(g)
-            if g < GROUPS - 1:
-                @pl.when(i == tail)
-                def _():
-                    give(g)
+            a_re, a_im = ebuf[0, band, :], ebuf[1, band, :]
+            xacc[0, band, lanes] += dot(a_re, b_re)
+            xacc[1, band, lanes] += dot(a_im, b_im)
+            xacc[2, band, lanes] += dot(a_re + a_im, b_sum)
+            if h == 1 or g < GROUPS - 1:
+                give(h, g)
 
     def right_step(i):
+        @pl.when(helps & (i == tail))
+        def _():
+            for k in range(LAG + 1):
+                lent_step(i - LAG + k)
+            give(0, GROUPS - 1)
+
         for n in range(2):
             s = jnp.where(z < rows // 2, 1 - n, n)
 
             @pl.when(present(s) & jnp.logical_not(is_own(s)) & jnp.logical_not(at_end & is_far(s) & late(i)))
             def _():
-                for k in range(FINE):
-                    b_arrival(s, i * FINE + k).wait()
-
-                    @pl.when(goes(s, i))
-                    def _():
-                        relay(s, i * FINE + k, late(i).astype(jnp.int32),
-                              jnp.where(goes_up(s), z + 1, z - 1)).start()
-
-        @pl.when(helps & late(i))
-        def _():
-            extra_step(i)
+                onward = jnp.where(goes_up(s), z + 1, z - 1)
+                in_halves = late(i) & helps & is_far(s)
+                by_halves = late(i) & is_outer(s)
+
+                @pl.when(jnp.logical_not(in_halves))
+                def _():
+                    for k in range(FINE):
+                        b_arrival(s, i * FINE + k).wait()
+
+                        @pl.when(goes(s, i) & jnp.logical_not(by_halves))
+                        def _():
+                            relay(s, i * FINE + k, late(i).astype(jnp.int32), onward).start()
+
+                @pl.when(by_halves & (i == tail))
+                def _():
+                    for h in range(2):
+                        half_relay(s, h, onward).start()
+
+                @pl.when(in_halves)
+                def _():
+                    ref = bbuf.at[s, i - kept, :, late_span, :]
+                    pltpu.make_async_copy(ref, ref, brecv.at[s, kept * FINE + i - kept]).wait()
+
+        @pl.when(helps & (i == kept))
+        def _():
+            extra_step(0)
 
         @pl.when(lends & (i == 0))
         def _():
@@ -447,7 +470,7 @@
         def _():
             multiply(abuf.at[1 - y], 1 - y, i)
 
-        @pl.when(helps & (i >= LAG))
+        @pl.when(helps & (i >= LAG) & (i < tail))
         def _():
             lent_step(i - LAG)
 
@@ -495,11 +518,7 @@
 
     @pl.when(helps)
     def _():
-        def lent_rest(i, carry):
-            lent_step(i)
-            return carry
-        lax.fori_loop(CHUNKS - LAG, CHUNKS, lent_rest, 0)
-        give(GROUPS - 1)
+        extra_step(1)
 
     def gather(b, carry):
         band = band_of(b)

time: 109 us -> 107 us (0.982); the launches traced: 109 us -> 106 us
  Pallas kernels: 108 us -> 105 us
    pallas_call x1, Pallas kernels: 108 us -> 105 us  [lent_product(): pl.pallas_call(functools.partial(kernel, rows), out_shape=[pltpu.VMEM(blo...]
where the time goes in v5:
time: 107 us; the launch traced here: 106 us
  Pallas kernels  105 us (98%)
    pallas_call x1, Pallas kernels, lent_product(): pl.pallas_call(functools.partial(kernel, rows), out_shape=[pltpu.VMEM(blo...  105 us

profile of v5, /device:TPU:0, one launch (start us, length us, event | category | flops | bytes accessed | tf_op | source)
XLA Modules:
  0.0 105.6 jit_solution(12512554633084142880)
XLA Ops:
  0.0 104.8 %shard_map.28 = (f32[2,256,128]{2,1,0:T(8,128)S(1)}, f32[2,256,128]{2,1,0:T(8,128)S(1)}) custom-call(f32[2,256,4096]{2,1,0:T(8,128)} %left.1, f32[2,4096,128]{2,1,0:T(8,128)} %right.1), custom_call_target="tpu_custom_call" | custom-call | tf_op jit(solution)/shard_map/pallas_call | solution.py:597
  104.9 0.7 add.3

commit v6 on v5

--- a/solution.py
+++ b/solution.py
@@ -197,6 +197,7 @@
         src_ref=abuf.at[1 - y, :, :, late_span], dst_ref=ebuf,
         send_sem=esem.at[0], recv_sem=esem.at[1], **other(row=inward))
 
+    defers = jnp.logical_not(at_end | helps)
     yields = at_end & jnp.logical_not(lends) & (y == lent_slot)
     sends_up = (z < last) & (z != last - 1)
     sends_down = (z > 0) & (z != 1)
@@ -225,7 +226,7 @@
             def _():
                 b_copy(i * FINE + k, 1, z - 1).start()
 
-        @pl.when(jnp.logical_not(yields | lends_own) & jnp.logical_not(lends_relayed & late(i)))
+        @pl.when(jnp.logical_not(yields | lends_own | defers) & jnp.logical_not(lends_relayed & late(i)))
         def _():
             y_copy(i).start()
 
@@ -259,11 +260,13 @@
             x_own(i)
             return carry
         lax.fori_loop(0, CHUNKS, lend, 0)
+
+    @pl.when(lends_own | helps)
+    def _():
         y_sent(0).wait_send()
         pl.semaphore_signal(turn, inc=1, **other(**partner))
 
-    @pl.when(yields)
-    def _():
+    def take_turn():
         pl.semaphore_wait(turn, 1)
 
         def cross(i, carry):
@@ -271,6 +274,10 @@
             return carry
         lax.fori_loop(0, CHUNKS, cross, 0)
 
+    @pl.when(yields)
+    def _():
+        take_turn()
+
     own_copy.wait()
 
     @pl.when(c == parity)
@@ -288,11 +295,11 @@
             src_ref=ref, dst_ref=ref, send_sem=rsend.at[s, part], recv_sem=brecv.at[s, u],
             **other(row=row))
 
-    def half_relay(s, h, row):
-        ref = bbuf.at[s, h, :, late_span, :]
+    def half_relay(s, n, row):
+        ref = bbuf.at[s, (1 - c + n) % 2, :, late_span, :]
         return pltpu.make_async_remote_copy(
             src_ref=ref, dst_ref=ref, send_sem=rsend.at[s, 1],
-            recv_sem=brecv.at[s, kept * FINE + h], **other(row=row))
+            recv_sem=brecv.at[s, kept * FINE + n], **other(row=row))
 
     def relayed(s, part):
         start, size = ((0, kept) if part == 0 else (kept, EXTRA))
@@ -390,10 +397,8 @@
         for k in range(per):
             lend_back(h, g * per + k).start()
 
-    def extra_step(h):
-        if h == 0:
-            e_own.wait_recv()
-
+    def extra_step(n):
+        h = (1 - c + n) % 2
         b_re, b_im = (bbuf[1 - z // 2, h, k, late_span, :] for k in range(2))
         b_sum = b_re + b_im
         lanes = half(h)
@@ -404,18 +409,67 @@
             xacc[0, band, lanes] += dot(a_re, b_re)
             xacc[1, band, lanes] += dot(a_im, b_im)
             xacc[2, band, lanes] += dot(a_re + a_im, b_sum)
-            if h == 1 or g < GROUPS - 1:
+            if g < GROUPS - 1:
                 give(h, g)
 
+    def banded(h, b):
+        first, second, third = (acc[k, band_of(b), half(h)] for k in range(3))
+        return first - second, third - first - second
+
+    def to_partner(b):
+        return pltpu.make_async_remote_copy(
+            src_ref=pout.at[:, band_of(b)], dst_ref=pin.at[:, band_of(b)],
+            send_sem=psend, recv_sem=precv.at[b], **other(**partner))
+
+    def hand(b, carry):
+        pout[0, band_of(b)], pout[1, band_of(b)] = banded(1 - c, b)
+        to_partner(b).start()
+        return carry
+
+    def half_wait(n):
+        s = 1 - z // 2
+        ref = bbuf.at[s, (1 - c + n) % 2, :, late_span, :]
+        pltpu.make_async_copy(ref, ref, brecv.at[s, kept * FINE + n]).wait()
+
+    def half_product(n):
+        s = 1 - z // 2
+        h = (1 - c + n) % 2
+        a_re, a_im = abuf[s, 0, :, late_span], abuf[s, 1, :, late_span]
+        b_re, b_im = (bbuf[s, h, k, late_span, :] for k in range(2))
+        lanes = half(h)
+        acc[0, :, lanes] += dot(a_re, b_re)
+        acc[1, :, lanes] += dot(a_im, b_im)
+        acc[2, :, lanes] += dot(a_re + a_im, b_re + b_im)
+
+    def half_step(i):
+        @pl.when(i == kept)
+        def _():
+            for k in range(kept, CHUNKS):
+                y_arrival(k).wait()
+            e_own.wait_recv()
+            half_wait(0)
+            extra_step(0)
+            half_product(0)
+            accumulate(abuf.at[z // 2], z // 2, late_span)
+            lax.fori_loop(0, BANDS, hand, 0)
+
+        @pl.when(i == tail)
+        def _():
+            half_wait(1)
+            extra_step(1)
+            lent_step(i - LAG)
+            lent_step(i)
+            for h in range(2):
+                give(h, GROUPS - 1)
+            half_product(1)
+
     def right_step(i):
-        @pl.when(helps & (i == tail))
-        def _():
-            for k in range(LAG + 1):
-                lent_step(i - LAG + k)
-            give(0, GROUPS - 1)
-
-        for n in range(2):
-            s = jnp.where(z < rows // 2, 1 - n, n)
+        @pl.when(defers & (i == kept))
+        def _():
+            take_turn()
+
+        for order in range(2):
+            s = jnp.where(z < rows // 2, 1 - order, order)
 
             @pl.when(present(s) & jnp.logical_not(is_own(s)) & jnp.logical_not(at_end & is_far(s) & late(i)))
             def _():
@@ -434,17 +488,12 @@
 
                 @pl.when(by_halves & (i == tail))
                 def _():
-                    for h in range(2):
-                        half_relay(s, h, onward).start()
-
-                @pl.when(in_halves)
-                def _():
-                    ref = bbuf.at[s, i - kept, :, late_span, :]
-                    pltpu.make_async_copy(ref, ref, brecv.at[s, kept * FINE + i - kept]).wait()
-
-        @pl.when(helps & (i == kept))
-        def _():
-            extra_step(0)
+                    for n in range(2):
+                        half_relay(s, n, onward).start()
+
+        @pl.when(helps & late(i))
+        def _():
+            half_step(i)
 
         @pl.when(lends & (i == 0))
         def _():
@@ -452,12 +501,12 @@
                 b_arrival(lent_slot, u).wait()
             accumulate(abuf.at[lent_slot], lent_slot, pl.ds(0, fill))
 
-        @pl.when(present(y))
+        @pl.when(present(y) & jnp.logical_not(helps & late(i)))
         def _():
             multiply(abuf.at[y], y, i)
 
     def left_step(i):
-        @pl.when(jnp.logical_not(lends_relayed | (lends_own & late(i))))
+        @pl.when(jnp.logical_not(lends_relayed | ((lends_own | helps) & late(i))))
         def _():
             y_arrival(i).wait()
 
@@ -466,7 +515,7 @@
             y_piece_arrival(i).wait()
             x_relay(i)
 
-        @pl.when(present(1 - y))
+        @pl.when(present(1 - y) & jnp.logical_not(helps & late(i)))
         def _():
             multiply(abuf.at[1 - y], 1 - y, i)
 
@@ -495,30 +544,14 @@
 
     lax.fori_loop(0, 2 * CHUNKS, work, 0)
 
-    def banded(h, b):
-        first, second, third = (acc[k, band_of(b), half(h)] for k in range(3))
-        return first - second, third - first - second
-
-    def to_partner(b):
-        return pltpu.make_async_remote_copy(
-            src_ref=pout.at[:, band_of(b)], dst_ref=pin.at[:, band_of(b)],
-            send_sem=psend, recv_sem=precv.at[b], **other(**partner))
-
     def to_copy(b):
         return pltpu.make_async_remote_copy(
             src_ref=qout.at[:, band_of(b)], dst_ref=qin.at[:, band_of(b)],
             send_sem=qsend, recv_sem=qrecv, **other(**copy_x))
 
-    def hand(b, carry):
-        pout[0, band_of(b)], pout[1, band_of(b)] = banded(1 - c, b)
-        to_partner(b).start()
-        return carry
-
-    lax.fori_loop(0, BANDS, hand, 0)
-
-    @pl.when(helps)
-    def _():
-        extra_step(1)
+    @pl.when(jnp.logical_not(helps))
+    def _():
+        lax.fori_loop(0, BANDS, hand, 0)
 
     def gather(b, carry):
         band = band_of(b)
@@ -556,7 +589,7 @@
             src_ref=ref, dst_ref=ref, send_sem=bsend.at[3], recv_sem=bown.at[1],
             **other(**partner)).wait_send()
 
-    @pl.when(jnp.logical_not(lends_own))
+    @pl.when(jnp.logical_not(lends_own | helps))
     def _():
         y_sent(0).wait_send()
 

time: 107 us -> 107 us (level); the launches traced: 106 us -> 107 us
  Pallas kernels: 105 us -> 107 us
    pallas_call x1, Pallas kernels: 105 us -> 107 us  [lent_product(): pl.pallas_call(functools.partial(kernel, rows), out_shape=[pltpu.VMEM(blo...]
where the time goes in v6:
time: 107 us
  Pallas kernels  107 us (100%)
    pallas_call x1, Pallas kernels, lent_product(): pl.pallas_call(functools.partial(kernel, rows), out_shape=[pltpu.VMEM(blo...  107 us

profile of v6, /device:TPU:0, one launch (start us, length us, event | category | flops | bytes accessed | tf_op | source)
XLA Modules:
  0.0 107.3 jit_solution(16851961204950431839)
XLA Ops:
  0.0 106.6 %shard_map.28 = (f32[2,256,128]{2,1,0:T(8,128)S(1)}, f32[2,256,128]{2,1,0:T(8,128)S(1)}) custom-call(f32[2,256,4096]{2,1,0:T(8,128)} %left.1, f32[2,4096,128]{2,1,0:T(8,128)} %right.1), custom_call_target="tpu_custom_call" | custom-call | tf_op jit(solution)/shard_map/pallas_call | solution.py:630
  106.6 0.7 add.3

commit v7 on v6

--- a/solution.py
+++ b/solution.py
@@ -505,6 +505,10 @@
         def _():
             multiply(abuf.at[y], y, i)
 
+        @pl.when(lends_relayed & (i == kept - 1))
+        def _():
+            lax.fori_loop(0, BANDS, hand, 0)
+
     def left_step(i):
         @pl.when(jnp.logical_not(lends_relayed | ((lends_own | helps) & late(i))))
         def _():
@@ -518,6 +522,10 @@
         @pl.when(present(1 - y) & jnp.logical_not(helps & late(i)))
         def _():
             multiply(abuf.at[1 - y], 1 - y, i)
+
+        @pl.when(lends_own & (i == kept - 1))
+        def _():
+            lax.fori_loop(0, BANDS, hand, 0)
 
         @pl.when(helps & (i >= LAG) & (i < tail))
         def _():
@@ -549,7 +557,7 @@
             src_ref=qout.at[:, band_of(b)], dst_ref=qin.at[:, band_of(b)],
             send_sem=qsend, recv_sem=qrecv, **other(**copy_x))
 
-    @pl.when(jnp.logical_not(helps))
+    @pl.when(jnp.logical_not(helps | lends))
     def _():
         lax.fori_loop(0, BANDS, hand, 0)
 

time: 107 us -> 107 us (level)
  no operation moved by 1% of the time
where the time goes in v7:
time: 107 us
  Pallas kernels  107 us (100%)
    pallas_call x1, Pallas kernels, lent_product(): pl.pallas_call(functools.partial(kernel, rows), out_shape=[pltpu.VMEM(blo...  107 us

profile of v7, /device:TPU:0, one launch (start us, length us, event | category | flops | bytes accessed | tf_op | source)
XLA Modules:
  0.0 107.3 jit_solution(9460892205616030700)
XLA Ops:
  0.0 106.5 %shard_map.28 = (f32[2,256,128]{2,1,0:T(8,128)S(1)}, f32[2,256,128]{2,1,0:T(8,128)S(1)}) custom-call(f32[2,256,4096]{2,1,0:T(8,128)} %left.1, f32[2,4096,128]{2,1,0:T(8,128)} %right.1), custom_call_target="tpu_custom_call" | custom-call | tf_op jit(solution)/shard_map/pallas_call | solution.py:638
  106.5 0.7 add.3

commit v8 on v5

--- a/solution.py
+++ b/solution.py
@@ -414,6 +414,10 @@
                 lent_step(i - LAG + k)
             give(0, GROUPS - 1)
 
+        @pl.when(helps & is_own(y))
+        def _():
+            multiply(abuf.at[y], y, i)
+
         for n in range(2):
             s = jnp.where(z < rows // 2, 1 - n, n)
 
@@ -452,7 +456,7 @@
                 b_arrival(lent_slot, u).wait()
             accumulate(abuf.at[lent_slot], lent_slot, pl.ds(0, fill))
 
-        @pl.when(present(y))
+        @pl.when(present(y) & jnp.logical_not(helps & is_own(y)))
         def _():
             multiply(abuf.at[y], y, i)
 

time: 107 us -> 107 us (level)
  no operation moved by 1% of the time
where the time goes in v8:
time: 107 us; the launch traced here: 106 us
  Pallas kernels  105 us (98%)
    pallas_call x1, Pallas kernels, lent_product(): pl.pallas_call(functools.partial(kernel, rows), out_shape=[pltpu.VMEM(blo...  105 us

profile of v8, /device:TPU:0, one launch (start us, length us, event | category | flops | bytes accessed | tf_op | source)
XLA Modules:
  0.0 105.6 jit_solution(6259963825667972681)
XLA Ops:
  0.0 104.9 %shard_map.28 = (f32[2,256,128]{2,1,0:T(8,128)S(1)}, f32[2,256,128]{2,1,0:T(8,128)S(1)}) custom-call(f32[2,256,4096]{2,1,0:T(8,128)} %left.1, f32[2,4096,128]{2,1,0:T(8,128)} %right.1), custom_call_target="tpu_custom_call" | custom-call | tf_op jit(solution)/shard_map/pallas_call | solution.py:601
  104.9 0.7 add.3
